TPU v7x, 32 devices: a whole 2x2x4 slice. The times are simulated.
32 devices in a mesh: seq: 8 (over z, y), head: 4 (over x, core).
Axes of the slice: x: 2, y: 2, z: 4, core: 2. Of those that a mesh axis runs over, the one named last changes fastest.
Arguments:
- hidden: bfloat16 [4096, 8192], P('seq', 'head'), may hold values from -6 to 6
- gain: float32 [8192], replicated, may hold values from 0.25 to 1.75
- key_matrix: bfloat16 [8192, 512], P(None, 'head'), may hold values from -0.0625 to 0.0625
- value_matrix: bfloat16 [8192, 512], P(None, 'head'), may hold values from -0.0625 to 0.0625
- queries: bfloat16 [64, 4096], P(None, 'head'), may hold values from -360 to 360
- window_len: int32 [4], P('head'), may hold values from 16 to 64, as said below
- kernel_width: int32 [4], P('head'), may hold values from 1 to 15, as said below
- kept_block_count: int32 [4], P('head'), may hold values from 1 to 16
Outputs:
- block_scores: float32 [4, 32], P('head', 'seq')
- kept_fraction: float32 [4], P('head')
Inputs may be any that keep to these rules, and one draw needn't show every extreme that they name: `window_len`: at least one key-value head uses all 64 window queries. `kernel_width`: odd; at least one key-value head has width 15.
All inputs are finite; a program needn't handle non-finite values.
Results may differ from a plain program's by a relative error of at most 0.0112.
The roundings to bfloat16 on the way count: a program that leaves them out, or rounds other values in their place, can miss the bound.
Values may be sent and summed in bfloat16 or wider, within the bound.
No kernel may reach another device: no remote copies, remote signals or barrier semaphores. Data moves between devices by JAX's collectives and lax.ppermute only.
A program may use at most 128 MiB of HBM per device.

v0:
```python
import jax
import jax.numpy as jnp
from jax import lax
from jax.sharding import PartitionSpec as P

BLK = 128
KERNEL_LIMIT = 15


def with_halo(x, sides, width):
    for axis, dim in sides:
        count, length = (lax.axis_size(axis), x.shape[dim])
        up = [(i, (i + 1) % count) for i in range(count - 1)]
        down = [(j, i) for i, j in up]
        last = lax.slice_in_dim(x, length - width, length, axis=dim)
        leading = lax.slice_in_dim(x, 0, width, axis=dim)
        before = lax.ppermute(last, axis, up)
        after = lax.ppermute(leading, axis, down)
        x = jnp.concatenate([before, x, after], axis=dim)
    return x


def rotate(raw, positions):
    half = raw.shape[1] // 2
    freq = 500000.0 ** (-(jnp.arange(half).astype(jnp.float32) * 2.0) / raw.shape[1])
    angle = positions[:, None] * freq[None, :]
    leading_part = raw[:, :half]
    trailing_part = raw[:, half:]
    return jnp.concatenate(
        [
            leading_part * jnp.cos(angle) - trailing_part * jnp.sin(angle),
            trailing_part * jnp.cos(angle) + leading_part * jnp.sin(angle),
        ],
        axis=1,
    )


def local(
    hidden, gain, key_matrix, value_matrix, queries, window_len, kernel_width, kept_block_count
):
    tok_rows = hidden.shape[0]
    full_width = gain.shape[0]
    head_size = key_matrix.shape[1]
    floats = hidden.astype(jnp.float32)
    sumsq = lax.psum(jnp.sum(floats * floats, axis=1), "head")
    inv_rms = lax.rsqrt(sumsq / full_width + 1e-05)
    joined = jnp.concatenate([key_matrix, value_matrix], axis=1)
    normed = (
        lax.all_gather(hidden, "head", axis=1, tiled=True).astype(jnp.float32) * gain[None, :]
    ).astype(jnp.bfloat16)
    projected = jnp.dot(normed, joined, preferred_element_type=jnp.float32)
    projected = projected * inv_rms[:, None]
    tok_index = lax.axis_index("seq") * tok_rows + jnp.arange(tok_rows)
    positions = tok_index.astype(jnp.float32)
    keys = rotate(projected[:, :head_size], positions).astype(jnp.bfloat16)
    vmag = jnp.mean(jnp.abs(projected[:, head_size:]), axis=1)
    window = queries.shape[0]
    group_heads = queries.shape[1] // head_size
    query_rows = queries.reshape(window * group_heads, head_size)
    scores = lax.dot_general(
        query_rows, keys, (((1,), (1,)), ((), ())), preferred_element_type=jnp.float32
    ) * head_size ** (-0.5)
    total_tokens = tok_rows * lax.axis_size("seq")
    limit = jnp.repeat(total_tokens - window + jnp.arange(window), group_heads)
    allowed = tok_index[None, :] <= limit[:, None]
    scores = jnp.where(allowed, scores, jnp.float32(-1e30))
    local_top = jnp.max(scores, axis=1)
    row_top = lax.pmax(local_top, "seq")
    expo = jnp.exp(scores - row_top[:, None])
    row_total = lax.psum(jnp.sum(expo, axis=1), "seq")
    rescale = jnp.ones_like(row_total)
    used = (jnp.arange(window) >= window - window_len[0]).astype(jnp.float32)
    row_weight = jnp.repeat(used, group_heads) * rescale / row_total
    column = jnp.dot(row_weight, expo, precision=lax.Precision.HIGHEST) * vmag
    reach = (KERNEL_LIMIT - 1) // 2
    padded = with_halo(column, (("seq", 0),), reach)
    kernel_halfspan = (kernel_width[0] - 1) // 2
    pooled = column
    for shift in range(1, reach + 1):
        wider = jnp.maximum(
            jnp.maximum(pooled, padded[reach + shift : reach + shift + tok_rows]),
            padded[reach - shift : reach - shift + tok_rows],
        )
        pooled = jnp.where(shift <= kernel_halfspan, wider, pooled)
    local_blocks = jnp.sum(pooled.reshape(tok_rows // BLK, BLK), axis=1)[None, :]
    everything = lax.all_gather(local_blocks, "seq", axis=1, tiled=True)[0]
    ordered = -jnp.sort(-everything)
    ranks = jnp.arange(ordered.shape[0])
    kept = jnp.sum(jnp.where(ranks < kept_block_count[0], ordered, jnp.float32(0.0)))
    fraction = (kept / jnp.sum(ordered)).reshape(1)
    return (local_blocks, fraction)


def solution(mesh):
    return jax.shard_map(
        local,
        mesh=mesh,
        in_specs=(
            P("seq", "head"),
            P(),
            P(None, "head"),
            P(None, "head"),
            P(None, "head"),
            P("head"),
            P("head"),
            P("head"),
        ),
        out_specs=(P("head", "seq"), P("head")),
        check_vma=False,
    )
```

profile of v0, /device:TPU:0, one launch (start us, length us, event | category | flops | bytes accessed | tf_op | source)
XLA Modules:
  0.0 157.1 jit_solution(7609627779435552544)
XLA Ops:
  7.2 0.0 copy-start.1
  7.2 0.0 all-gather.3.cloned.1.call-start
  7.2 0.7 all-gather.3.cloned.1.call-update
  8.6 1.0 reshape.43
  9.6 0.1 broadcast_in_dim.24
  9.6 0.1 le.16
  10.4 0.1 broadcast_in_dim.23
  10.5 0.1 reshape.42
  11.3 1.2 dynamic-slice
  13.1 2.1 %multiply_reduce_fusion = f32[512]{0:T(512)S(1)} fusion(bf16[512,2048]{1,0:T(8,128)(2,1)} %param.8), kind=kLoop, calls=%fused_computation.6 | loop fusion | flops 3145216 | bytes 2099200 | tf_op jit(solution)/shard_map/reduce_sum | solution.py:45
  15.2 8.4 %psum.14 = f32[512]{0:T(512)S(1)} all-reduce(f32[512]{0:T(512)S(1)} %multiply_reduce_fusion), channel_id=1, replica_groups=mesh['seq'=8,'head'=4] {'head'}, use_global_device_ids=true, to_apply=%region_1.0 | all-reduce | flops 512 | bytes 4096 | tf_op jit(solution)/shard_map/psum | solution.py:45
  23.6 46.9 %all-gather.3.cloned.1.call-done = bf16[512,8192]{1,0:T(8,128)(2,1)} async-done(((bf16[512,2048]{1,0:T(8,128)(2,1)}), bf16[512,8192]{1,0:T(8,128)(2,1)}) %all-gather.3.cloned.1.call-update) | async-done | bytes 8388624 | tf_op jit(solution)/shard_map/all_gather | solution.py:49
  70.6 6.3 %fusion.7 = f32[512,256]{0,1:T(8,128)S(1)} fusion(bf16[8192,128]{1,0:T(8,128)(2,1)S(1)} %copy-done.1, bf16[8192,128]{1,0:T(8,128)(2,1)} %param.10, bf16[512,8192]{1,0:T(8,128)(2,1)} %all-gather.3.cloned.1.call-done, f32[8192]{0:T(1024)S(1)} %copy-done.2, f32[512]{0:T(512)S(1)} %add_rsqrt_fusion), kind=kOutput, calls=%fused_computation.10 | convolution fusion | flops 2168586240 | bytes 13142016 | tf_op jit(solution)/shard_map/dot_general | solution.py:51
  77.0 0.6 fusion.19
  77.5 0.4 fusion.31
  77.9 21.4 %pmax.7 = f32[512]{0:T(512)S(1)} all-reduce(f32[512]{0:T(512)S(1)} %get-tuple-element.13), channel_id=1, replica_groups=mesh['seq'=8,'head'=4] {'seq'}, use_global_device_ids=true, to_apply=%region_3.4 | all-reduce | flops 512 | bytes 4096 | tf_op jit(solution)/shard_map/pmax | solution.py:68
  99.3 0.2 fusion.11
  99.5 17.1 %psum.15 = f32[512]{0:T(512)S(1)} all-reduce(f32[512]{0:T(512)S(1)} %fusion.11), channel_id=1, replica_groups=mesh['seq'=8,'head'=4] {'seq'}, use_global_device_ids=true, to_apply=%region_5.6 | all-reduce | flops 512 | bytes 4096 | tf_op jit(solution)/shard_map/psum | solution.py:70
  116.6 1.0 fusion.10
  117.6 0.1 fusion.30
  117.7 1.3 collective-permute-start
  119.0 4.5 %collective-permute-start.1 = (f32[7]{0:T(128)S(1)}, f32[7]{0:T(128)S(1)}, u32[]{:S(2)}, u32[]{:S(2)}) collective-permute-start(f32[7]{0:T(128)S(1)} %get-tuple-element.12), channel_id=1, source_target_pairs={{0,4},{4,8},{8,12},{12,16},{16,20},{20,24},{24,28},{1,5},{5,9},{9,... | collective-permute-start | bytes 92 | tf_op jit(solution)/shard_map/ppermute | solution.py:17
  123.6 0.0 collective-permute-done
  123.6 1.3 collective-permute-done.1
  124.8 0.1 pad_maximum_fusion
  124.9 0.2 bitcast_reduce_fusion
  125.1 0.0 copy-start
  125.1 0.2 dynamic-update-slice
  125.4 20.0 %all-reduce = f32[32]{0:T(128)S(1)} all-reduce(f32[32]{0:T(128)S(1)} %dynamic-update-slice), channel_id=2, replica_groups=mesh['seq'=8,'head'=4] {'seq'}, use_global_device_ids=true, to_apply=%add | all-reduce | flops 32 | bytes 256
  145.4 1.6 %sort.15 = (f32[32]{0:T(128)S(1)}, s32[32]{0:T(128)}) sort(f32[32]{0:T(128)S(1)} %neg.23, s32[32]{0:T(128)S(1)} %iota.29), dimensions={0}, to_apply=%region_8.9 | sort | flops 160 | bytes 512 | tf_op jit(solution)/shard_map/jit(sort)/sort | solution.py:87
  147.0 0.7 fusion.29
  149.1 0.0 copy-done
  (15 shorter events, 0.1 us)
Async XLA Ops:
  7.2 63.4 %copy-start.1 = (bf16[8192,128]{1,0:T(8,128)(2,1)S(1)}, bf16[8192,128]{1,0:T(8,128)(2,1)}, u32[]{:S(2)}) copy-start(bf16[8192,128]{1,0:T(8,128)(2,1)} %param.11) | copy-start | bytes 6291460
  7.2 63.4 %copy-start.2 = (f32[8192]{0:T(1024)S(1)}, f32[8192]{0:T(1024)}, u32[]{:S(2)}) copy-start(f32[8192]{0:T(1024)} %param.9) | copy-start | bytes 98308
  7.2 63.4 %all-gather.3.cloned.1.call-start = ((), (), s32[]{:S(2)}) async-start(), calls=%async_computation | async-start | bytes 10485760 | tf_op jit(solution)/shard_map/all_gather | solution.py:49
  117.7 5.9 %collective-permute-start = (f32[7]{0:T(128)S(1)}, f32[7]{0:T(128)S(1)}, u32[]{:S(2)}, u32[]{:S(2)}) collective-permute-start(f32[7]{0:T(128)S(1)} %get-tuple-element.11), channel_id=1, source_target_pairs={{4,0},{8,4},{12,8},{16,12},{20,16},{24,20},{28,24},{5,1},{9,5},{13... | collective-permute-start | bytes 92 | tf_op jit(solution)/shard_map/ppermute | solution.py:18
  119.0 5.8 %collective-permute-start.1 = (f32[7]{0:T(128)S(1)}, f32[7]{0:T(128)S(1)}, u32[]{:S(2)}, u32[]{:S(2)}) collective-permute-start(f32[7]{0:T(128)S(1)} %get-tuple-element.12), channel_id=1, source_target_pairs={{0,4},{4,8},{8,12},{12,16},{16,20},{20,24},{24,28},{1,5},{5,9},{9,... | collective-permute-start | bytes 92 | tf_op jit(solution)/shard_map/ppermute | solution.py:17
  125.1 24.0 %copy-start = (f32[4]{0:T(128)}, f32[4]{0:T(128)S(1)}, u32[]{:S(2)}) copy-start(f32[4]{0:T(128)S(1)} %bitcast_reduce_fusion) | copy-start | bytes 52
Sparse Core Ops, SparseCore 0:
  9.6 60.9 all-gather.2
where the time goes:
time: 157 us
  blocking collectives  66.9 us (43%)
  waiting for transfers between devices  48.9 us (31%)
  between operations  19.3 us (12%)
  matrix products  7.68 us (5%)
  starting transfers between devices  5.88 us (4%)
  other arithmetic  5.53 us (4%)
  local copies, waits for them, and re-layouts  2.88 us (2%)
    all_gather x1, waiting for transfers between devices, local(): lax.all_gather(hidden, 'head', axis=1, tiled=True).astype(jnp.float32)  46.9 us
    pmax x1, blocking collectives, local(): row_top = lax.pmax(local_top, 'seq')  21.4 us
    unnamed x1, blocking collectives  20 us
    psum x1, blocking collectives, local(): row_total = lax.psum(jnp.sum(expo, axis=1), 'seq')  17.1 us
    psum x1, blocking collectives, local(): sumsq = lax.psum(jnp.sum(floats * floats, axis=1), 'head')  8.37 us
    dot_general x1, matrix products, local(): projected = jnp.dot(normed, joined, preferred_element_type=jnp.float32)  6.35 us
    ppermute x1, starting transfers between devices, with_halo(): before = lax.ppermute(last, axis, up)  4.55 us
  transfers between devices with their start and end apart: 3, of which 2 were waited for; matrix products, arithmetic and copies ran while one was open for 3% of the time, Pallas kernels for 0%

commit v1 on v0

--- a/solution.py
+++ b/solution.py
@@ -67,7 +67,7 @@
     local_top = jnp.max(scores, axis=1)
     row_top = lax.pmax(local_top, "seq")
     expo = jnp.exp(scores - row_top[:, None])
-    row_total = lax.psum(jnp.sum(expo, axis=1), "seq")
+    row_total = jnp.sum(lax.all_gather(jnp.sum(expo, axis=1), "seq"), axis=0)
     rescale = jnp.ones_like(row_total)
     used = (jnp.arange(window) >= window - window_len[0]).astype(jnp.float32)
     row_weight = jnp.repeat(used, group_heads) * rescale / row_total

time: 157 us -> 166 us (1.057)
  blocking collectives: 66.9 us -> 75.3 us
    all_gather x0 -> x1, blocking collectives: none -> 26.1 us  [local(): row_total = jnp.sum(lax.all_gather(jnp.sum(expo, axis=1), 'seq'), axis=0)]
    psum x1 -> x0, blocking collectives: 17.1 us -> none  [local(): row_total = lax.psum(jnp.sum(expo, axis=1), 'seq')]
where the time goes in v1:
time: 166 us; the launch traced here: 165 us
  blocking collectives  75.3 us (45%)
  waiting for transfers between devices  48.9 us (29%)
  between operations  19.3 us (12%)
  matrix products  7.68 us (5%)
  starting transfers between devices  5.88 us (4%)
  other arithmetic  5.56 us (3%)
  local copies, waits for them, and re-layouts  2.88 us (2%)
    all_gather x1, waiting for transfers between devices, local(): lax.all_gather(hidden, 'head', axis=1, tiled=True).astype(jnp.float32)  46.9 us
    all_gather x1, blocking collectives, local(): row_total = jnp.sum(lax.all_gather(jnp.sum(expo, axis=1), 'seq'), axis=0)  26.1 us
    pmax x1, blocking collectives, local(): row_top = lax.pmax(local_top, 'seq')  21.4 us
    unnamed x1, blocking collectives  19.4 us
    psum x1, blocking collectives, local(): sumsq = lax.psum(jnp.sum(floats * floats, axis=1), 'head')  8.37 us
    dot_general x1, matrix products, local(): projected = jnp.dot(normed, joined, preferred_element_type=jnp.float32)  6.35 us
    ppermute x1, starting transfers between devices, with_halo(): before = lax.ppermute(last, axis, up)  4.55 us
  transfers between devices with their start and end apart: 3, of which 2 were waited for; matrix products, arithmetic and copies ran while one was open for 3% of the time, Pallas kernels for 0%

profile of v1, /device:TPU:0, one launch (start us, length us, event | category | flops | bytes accessed | tf_op | source)
XLA Modules:
  0.0 165.4 jit_solution(12819597643951956781)
XLA Ops:
  7.2 0.0 copy-start.1
  7.2 0.0 copy-start.2
  7.2 0.0 all-gather.5.cloned.1.call-start
  7.2 0.7 all-gather.5.cloned.1.call-update
  8.6 1.0 reshape.43
  9.6 0.1 broadcast_in_dim.24
  9.6 0.1 le.16
  10.4 0.1 broadcast_in_dim.23
  10.5 0.1 reshape.42
  11.3 1.2 dynamic-slice
  13.1 2.1 %multiply_reduce_fusion = f32[512]{0:T(512)S(1)} fusion(bf16[512,2048]{1,0:T(8,128)(2,1)} %param.8), kind=kLoop, calls=%fused_computation.6 | loop fusion | flops 3145216 | bytes 2099200 | tf_op jit(solution)/shard_map/reduce_sum | solution.py:45
  15.2 8.4 %psum.7 = f32[512]{0:T(512)S(1)} all-reduce(f32[512]{0:T(512)S(1)} %multiply_reduce_fusion), channel_id=1, replica_groups=mesh['seq'=8,'head'=4] {'head'}, use_global_device_ids=true, to_apply=%region_1.0 | all-reduce | flops 512 | bytes 4096 | tf_op jit(solution)/shard_map/psum | solution.py:45
  23.6 46.9 %all-gather.5.cloned.1.call-done = bf16[512,8192]{1,0:T(8,128)(2,1)} async-done(((bf16[512,2048]{1,0:T(8,128)(2,1)}), bf16[512,8192]{1,0:T(8,128)(2,1)}) %all-gather.5.cloned.1.call-update) | async-done | bytes 8388624 | tf_op jit(solution)/shard_map/all_gather | solution.py:49
  70.6 6.3 %fusion.7 = f32[512,256]{0,1:T(8,128)S(1)} fusion(bf16[8192,128]{1,0:T(8,128)(2,1)S(1)} %copy-done.1, bf16[8192,128]{1,0:T(8,128)(2,1)} %param.10, bf16[512,8192]{1,0:T(8,128)(2,1)} %all-gather.5.cloned.1.call-done, f32[8192]{0:T(1024)S(1)} %copy-done.2, f32[512]{0:T(512)S(1)} %add_rsqrt_fusion), kind=kOutput, calls=%fused_computation.10 | convolution fusion | flops 2168586240 | bytes 13142016 | tf_op jit(solution)/shard_map/dot_general | solution.py:51
  77.0 0.6 fusion.19
  77.5 0.4 fusion.31
  77.9 21.4 %pmax.7 = f32[512]{0:T(512)S(1)} all-reduce(f32[512]{0:T(512)S(1)} %get-tuple-element.13), channel_id=1, replica_groups=mesh['seq'=8,'head'=4] {'seq'}, use_global_device_ids=true, to_apply=%region_3.4 | all-reduce | flops 512 | bytes 4096 | tf_op jit(solution)/shard_map/pmax | solution.py:68
  99.3 0.2 fusion.11
  99.5 26.1 %all-gather.2 = f32[8,1,512]{2,1,0:T(1,128)S(1)} all-gather(f32[1,1,512]{2,1,0:T(1,128)S(1)} %bitcast.20), channel_id=2, replica_groups=mesh['seq'=8,'head'=4] {'seq'}, dimensions={0}, use_global_device_ids=true | all-gather | bytes 18432 | tf_op jit(solution)/shard_map/all_gather | solution.py:70
  125.7 1.0 fusion.10
  126.6 0.1 fusion.30
  126.7 1.3 collective-permute-start
  128.0 4.5 %collective-permute-start.1 = (f32[7]{0:T(128)S(1)}, f32[7]{0:T(128)S(1)}, u32[]{:S(2)}, u32[]{:S(2)}) collective-permute-start(f32[7]{0:T(128)S(1)} %get-tuple-element.12), channel_id=1, source_target_pairs={{0,4},{4,8},{8,12},{12,16},{16,20},{20,24},{24,28},{1,5},{5,9},{9,... | collective-permute-start | bytes 92 | tf_op jit(solution)/shard_map/ppermute | solution.py:17
  132.6 0.0 collective-permute-done
  132.6 1.3 collective-permute-done.1
  133.9 0.1 pad_maximum_fusion
  133.9 0.2 bitcast_reduce_fusion
  134.1 0.0 copy-start
  134.2 0.2 dynamic-update-slice
  134.4 19.4 %all-reduce = f32[32]{0:T(128)S(1)} all-reduce(f32[32]{0:T(128)S(1)} %dynamic-update-slice), channel_id=3, replica_groups=mesh['seq'=8,'head'=4] {'seq'}, use_global_device_ids=true, to_apply=%add | all-reduce | flops 32 | bytes 256
  153.8 1.6 sort.15
  155.4 0.7 fusion.29
  (16 shorter events, 0.1 us)
Async XLA Ops:
  7.2 63.4 %copy-start.1 = (bf16[8192,128]{1,0:T(8,128)(2,1)S(1)}, bf16[8192,128]{1,0:T(8,128)(2,1)}, u32[]{:S(2)}) copy-start(bf16[8192,128]{1,0:T(8,128)(2,1)} %param.11) | copy-start | bytes 6291460
  7.2 63.4 %copy-start.2 = (f32[8192]{0:T(1024)S(1)}, f32[8192]{0:T(1024)}, u32[]{:S(2)}) copy-start(f32[8192]{0:T(1024)} %param.9) | copy-start | bytes 98308
  7.2 63.4 %all-gather.5.cloned.1.call-start = ((), (), s32[]{:S(2)}) async-start(), calls=%async_computation | async-start | bytes 10485760 | tf_op jit(solution)/shard_map/all_gather | solution.py:49
  126.7 5.9 %collective-permute-start = (f32[7]{0:T(128)S(1)}, f32[7]{0:T(128)S(1)}, u32[]{:S(2)}, u32[]{:S(2)}) collective-permute-start(f32[7]{0:T(128)S(1)} %get-tuple-element.11), channel_id=1, source_target_pairs={{4,0},{8,4},{12,8},{16,12},{20,16},{24,20},{28,24},{5,1},{9,5},{13... | collective-permute-start | bytes 92 | tf_op jit(solution)/shard_map/ppermute | solution.py:18
  128.0 5.8 %collective-permute-start.1 = (f32[7]{0:T(128)S(1)}, f32[7]{0:T(128)S(1)}, u32[]{:S(2)}, u32[]{:S(2)}) collective-permute-start(f32[7]{0:T(128)S(1)} %get-tuple-element.12), channel_id=1, source_target_pairs={{0,4},{4,8},{8,12},{12,16},{16,20},{20,24},{24,28},{1,5},{5,9},{9,... | collective-permute-start | bytes 92 | tf_op jit(solution)/shard_map/ppermute | solution.py:17
  134.1 23.3 %copy-start = (f32[4]{0:T(128)}, f32[4]{0:T(128)S(1)}, u32[]{:S(2)}) copy-start(f32[4]{0:T(128)S(1)} %bitcast_reduce_fusion) | copy-start | bytes 52
Sparse Core Ops, SparseCore 0:
  9.6 60.9 all-gather.4
